TPU v7x, 32 devices: a whole 2x2x4 slice. The times are simulated.
32 devices in a mesh: gx: 8 (over y, x, core), gy: 4 (over z).
Axes of the slice: x: 2, y: 2, z: 4, core: 2. Of those that a mesh axis runs over, the one named last changes fastest.
Arguments:
- collocation: bfloat16 [3072, 16384], P(None, 'gx'), may hold values from -6 to 6
- density: bfloat16 [3072, 3072], P('gy'), may hold values from -0.109375 to 0.109375
- kernel: bfloat16 [16384, 8, 4, 512], P('gx', None, 'gy'), may hold values from -6.67572e-06 to 6.67572e-06
Outputs:
- exchange: float32 [3072, 3072], P('gx', 'gy')
All inputs are finite; a program needn't handle non-finite values.
Results may differ from a plain program's by a relative error of at most 0.008.
Values may be sent and summed in bfloat16 or wider, within the bound.
A program may use at most 448 MiB of HBM per device.

v0:
```python
import jax
import jax.numpy as jnp
from jax import lax
from jax.sharding import PartitionSpec as P


def local(collocation, density, kernel):
    piece_width = kernel.shape[3]
    column_group = lax.axis_index("gy")
    own_rows = jnp.dot(density, collocation, preferred_element_type=jnp.float32).astype(
        jnp.bfloat16
    )
    dense_block = lax.all_gather(own_rows, "gy", axis=0, tiled=True)
    own_piece = lax.dynamic_slice_in_dim(collocation, column_group * piece_width, piece_width, 1)
    kernel_tiles = kernel[:, :, 0, :]
    panel_rows = kernel_tiles.shape[0]
    gathered = lax.all_gather(own_piece, "gx", axis=1, tiled=True)
    products = lax.dot_general(
        dense_block, gathered, (((0,), (0,)), ((), ())), preferred_element_type=jnp.float32
    )
    coefficients = kernel_tiles.reshape(panel_rows, gathered.shape[1])
    weighted = (coefficients.astype(jnp.float32) * products).astype(jnp.bfloat16)
    chosen = gathered
    reduced_cols = lax.psum_scatter(
        lax.dot_general(
            chosen, weighted, (((1,), (1,)), ((), ())), preferred_element_type=jnp.float32
        ),
        "gy",
        scatter_dimension=0,
        tiled=True,
    ).astype(jnp.bfloat16)
    chosen = collocation
    return lax.psum_scatter(
        lax.dot_general(
            chosen, reduced_cols, (((1,), (1,)), ((), ())), preferred_element_type=jnp.float32
        ),
        "gx",
        scatter_dimension=0,
        tiled=True,
    )


def solution(mesh):
    return jax.shard_map(
        local,
        mesh=mesh,
        in_specs=(P(None, "gx"), P("gy", None), P("gx", None, "gy", None)),
        out_specs=P("gx", "gy"),
        check_vma=False,
    )
```

profile of v0, /device:TPU:0, one launch (start us, length us, event | category | flops | bytes accessed | tf_op | source)
XLA Modules:
  0.0 1016.0 jit_solution(8901126047309515792)
XLA Ops:
  6.5 0.0 all-gather.5.cloned.1.call-start
  6.5 15.4 %convolution_convert_fusion = bf16[768,2048]{1,0:T(8,128)(2,1)} fusion(bf16[768,3072]{1,0:T(8,128)(2,1)} %param.4, bf16[3072,2048]{1,0:T(8,128)(2,1)} %param.3), kind=kOutput, calls=%fused_computation.2 | convolution fusion | flops 9665249280 | bytes 20447232 | tf_op jit(solution)/shard_map/dot_general | solution.py:10
  22.0 0.0 all-gather.5.cloned.1.call-update
  22.0 0.0 all-gather.3.cloned.1.call-start
  22.0 3.8 constant_dynamic-slice_fusion
  25.8 0.0 all-gather.3.cloned.1.call-update
  25.9 0.0 reduce-scatter.3.cloned.1.call-start
  25.9 20.2 %copy.5 = f32[256,8,8,512]{3,1,2,0:T(8,128)} copy(bf16[256,8,8,512]{3,2,1,0:T(8,128)(2,1)} %bitcast.15) | data formatting | bytes 50331648
  46.1 197.0 %all-gather.5.cloned.1.call-done = bf16[3072,2048]{1,0:T(8,128)(2,1)} async-done(((bf16[768,2048]{1,0:T(8,128)(2,1)}), bf16[3072,2048]{1,0:T(8,128)(2,1)}) %all-gather.5.cloned.1.call-update) | async-done | bytes 12582928 | tf_op jit(solution)/shard_map/all_gather | solution.py:13
  243.1 130.3 %all-gather.3.cloned.1.call-done = bf16[3072,4096]{1,0:T(8,128)(2,1)} async-done(((bf16[3072,512]{1,0:T(8,128)(2,1)}), bf16[3072,4096]{1,0:T(8,128)(2,1)}) %all-gather.3.cloned.1.call-update) | async-done | bytes 25165840 | tf_op jit(solution)/shard_map/all_gather | solution.py:17
  373.3 62.4 %multiply_convert_fusion = bf16[2048,4096]{1,0:T(8,128)(2,1)} fusion(f32[2048,4096]{1,0:T(8,128)} %bitcast.14, bf16[3072,2048]{1,0:T(8,128)(2,1)} %all-gather.5.cloned.1.call-done, bf16[3072,4096]{1,0:T(8,128)(2,1)} %all-gather.3.cloned.1.call-done), kind=kOutput, calls=%fused_computation | convolution fusion | flops 51556384768 | bytes 88080384 | tf_op jit(solution)/shard_map/dot_general | solution.py:18
  435.7 61.0 %fusion.1 = f32[3072,2048]{1,0:T(8,128)} fusion(bf16[3072,4096]{1,0:T(8,128)(2,1)} %all-gather.3.cloned.1.call-done, bf16[2048,4096]{1,0:T(8,128)(2,1)} %multiply_convert_fusion), kind=kOutput, calls=%fused_computation.5 | convolution fusion | flops 51539607552 | bytes 67108864 | tf_op jit(solution)/shard_map/dot_general | solution.py:25
  496.7 0.0 reduce-scatter.3.cloned.1.call-update
  496.8 0.0 reduce-scatter.5.cloned.1.call-start
  496.8 414.3 %reduce-scatter.3.cloned.1.call-done = f32[768,2048]{1,0:T(8,128)} async-done(((f32[3072,2048]{1,0:T(8,128)}), f32[768,2048]{1,0:T(8,128)}) %reduce-scatter.3.cloned.1.call-update) | async-done | bytes 6291472 | tf_op jit(solution)/shard_map/reduce_scatter | solution.py:24
  911.1 16.9 %convolution_bitcast_fusion = f32[3072,768]{0,1:T(8,128)} fusion(bf16[3072,2048]{1,0:T(8,128)(2,1)} %param.3, f32[768,2048]{1,0:T(8,128)} %reduce-scatter.3.cloned.1.call-done), kind=kOutput, calls=%fused_computation.1 | convolution fusion | flops 9665249280 | bytes 28311552 | tf_op jit(solution)/shard_map/dot_general | solution.py:34
  928.0 0.0 reduce-scatter.5.cloned.1.call-update
  928.1 78.8 %reduce-scatter.5.cloned.1.call-done = f32[384,768]{0,1:T(8,128)} async-done(((f32[3072,768]{0,1:T(8,128)}), f32[384,768]{0,1:T(8,128)}) %reduce-scatter.5.cloned.1.call-update) | async-done | bytes 1179664 | tf_op jit(solution)/shard_map/reduce_scatter | solution.py:33
  1006.8 2.7 copy.4
Async XLA Ops:
  6.5 236.5 %all-gather.5.cloned.1.call-start = ((), (), s32[]{:S(2)}) async-start(), calls=%async_computation.3 | async-start | bytes 15728640 | tf_op jit(solution)/shard_map/all_gather | solution.py:13
  22.0 351.3 %all-gather.3.cloned.1.call-start = ((), (), s32[]{:S(2)}) async-start(), calls=%async_computation.2 | async-start | bytes 28311552 | tf_op jit(solution)/shard_map/all_gather | solution.py:17
  25.9 885.3 %reduce-scatter.3.cloned.1.call-start = ((), (), s32[]{:S(2)}) async-start(), calls=%async_computation.4 | async-start | bytes 31457280 | tf_op jit(solution)/shard_map/reduce_scatter | solution.py:24
  496.8 510.0 %reduce-scatter.5.cloned.1.call-start = ((), (), s32[]{:S(2)}) async-start(), calls=%async_computation.5 | async-start | bytes 10616832 | tf_op jit(solution)/shard_map/reduce_scatter | solution.py:33
Sparse Core Ops, SparseCore 0:
  22.1 220.8 all-gather.4
  244.9 128.3 all-gather.2
  496.9 414.1 reduce-scatter.2
  928.2 78.5 reduce-scatter.4
where the time goes:
time: 1020 us
  waiting for transfers between devices  820 us (80%)
  matrix products  156 us (15%)
  local copies, waits for them, and re-layouts  26.6 us (3%)
  between operations  13.1 us (1%)
    reduce_scatter x1, waiting for transfers between devices, local(): lax.psum_scatter(lax.dot_general(chosen, weighted, (((1,), (1,)), ((), ()...  414 us
    all_gather x1, waiting for transfers between devices, local(): dense_block = lax.all_gather(own_rows, 'gy', axis=0, tiled=True)  197 us
    all_gather x1, waiting for transfers between devices, local(): gathered = lax.all_gather(own_piece, 'gx', axis=1, tiled=True)  130 us
    reduce_scatter x1, waiting for transfers between devices, local(): lax.psum_scatter(lax.dot_general(chosen, reduced_cols, (((1,), (1,)), (()...  78.8 us
    dot_general x1, matrix products, local(): lax.dot_general(dense_block, gathered, (((0,), (0,)), ((), ())), preferre...  62.4 us
    dot_general x1, matrix products, local(): lax.dot_general(chosen, weighted, (((1,), (1,)), ((), ())), preferred_ele...  61 us
  transfers between devices with their start and end apart: 4, of which 4 were waited for; matrix products, arithmetic and copies ran while one was open for 2% of the time, Pallas kernels for 0%

commit v1 on v0

--- a/solution.py
+++ b/solution.py
@@ -10,7 +10,14 @@
     own_rows = jnp.dot(density, collocation, preferred_element_type=jnp.float32).astype(
         jnp.bfloat16
     )
-    dense_block = lax.all_gather(own_rows, "gy", axis=0, tiled=True)
+    devices = lax.axis_size("gy")
+    route = [(i, (i + 1) % devices) for i in range(devices)]
+    shards = [own_rows]
+    for stride in range(1, devices):
+        shards = [lax.ppermute(shards[0], "gy", route), *shards]
+    result = jnp.concatenate(shards, axis=0)
+    shift = (lax.axis_index("gy") + 1) * shards[-1].shape[0]
+    dense_block = jnp.roll(result, shift, axis=0)
     own_piece = lax.dynamic_slice_in_dim(collocation, column_group * piece_width, piece_width, 1)
     kernel_tiles = kernel[:, :, 0, :]
     panel_rows = kernel_tiles.shape[0]

time: 1020 us -> 909 us (0.89)
  waiting for transfers between devices: 820 us -> 683 us
  local copies, waits for them, and re-layouts: 26.6 us -> 53.8 us
    all_gather x1 -> x0, waiting for transfers between devices: 197 us -> none  [local(): dense_block = lax.all_gather(own_rows, 'gy', axis=0, tiled=True)]
    ppermute x0 -> x3, waiting for transfers between devices: none -> 192 us  [local(): shards = [lax.ppermute(shards[0], 'gy', route), *shards]]
    all_gather x1, waiting for transfers between devices: 130 us -> 0.01 us  [local(): gathered = lax.all_gather(own_piece, 'gx', axis=1, tiled=True)]
    unnamed x1 -> x12, local copies, waits for them, and re-layouts: 20.2 us -> 45.5 us
  transfers between devices with their start and end apart: 4 -> 6, of which waited for: 4 -> 5; matrix products, arithmetic and copies ran while one was open for 2% -> 7% of each run, Pallas kernels for 0% -> 0%
where the time goes in v1:
time: 909 us; the launch traced here: 908 us
  waiting for transfers between devices  683 us (75%)
  matrix products  155 us (17%)
  local copies, waits for them, and re-layouts  53.8 us (6%)
  between operations  13.1 us (1%)
    reduce_scatter x1, waiting for transfers between devices, local(): lax.psum_scatter(lax.dot_general(chosen, weighted, (((1,), (1,)), ((), ()...  412 us
    ppermute x3, waiting for transfers between devices, local(): shards = [lax.ppermute(shards[0], 'gy', route), *shards]  192 us
    reduce_scatter x1, waiting for transfers between devices, local(): lax.psum_scatter(lax.dot_general(chosen, reduced_cols, (((1,), (1,)), (()...  78.7 us
    dot_general x1, matrix products, local(): lax.dot_general(dense_block, gathered, (((0,), (0,)), ((), ())), preferre...  62.7 us
    dot_general x1, matrix products, local(): lax.dot_general(chosen, weighted, (((1,), (1,)), ((), ())), preferred_ele...  61 us
    unnamed x12, local copies, waits for them, and re-layouts  45.5 us
  transfers between devices with their start and end apart: 6, of which 5 were waited for; matrix products, arithmetic and copies ran while one was open for 7% of the time, Pallas kernels for 0%

profile of v1, /device:TPU:0, one launch (start us, length us, event | category | flops | bytes accessed | tf_op | source)
XLA Modules:
  0.0 908.1 jit_solution(16752154800002937877)
XLA Ops:
  6.5 3.8 constant_dynamic-slice_fusion
  10.3 0.0 reduce-scatter.3.cloned.1.call-start
  10.4 14.3 %convolution_convert_fusion = bf16[768,2048]{1,0:T(8,128)(2,1)S(1)} fusion(bf16[768,3072]{1,0:T(8,128)(2,1)} %param.4, bf16[3072,2048]{1,0:T(8,128)(2,1)} %param.3), kind=kOutput, calls=%fused_computation.3 | convolution fusion | flops 9665249280 | bytes 20447232 | tf_op jit(solution)/shard_map/dot_general | solution.py:10
  24.6 3.1 collective-permute-start
  27.7 70.1 %collective-permute-done = bf16[768,2048]{1,0:T(8,128)(2,1)S(1)} collective-permute-done((bf16[768,2048]{1,0:T(8,128)(2,1)S(1)}, bf16[768,2048]{1,0:T(8,128)(2,1)S(1)}, u32[]{:S(2)}, u32[]{:S(2)}) %collective-permute-start) | collective-permute-done | bytes 3145760 | tf_op jit(solution)/shard_map/ppermute | solution.py:17
  97.9 1.7 copy-done
  99.6 71.2 %collective-permute-done.1 = bf16[768,2048]{1,0:T(8,128)(2,1)} collective-permute-done((bf16[768,2048]{1,0:T(8,128)(2,1)S(1)}, bf16[768,2048]{1,0:T(8,128)(2,1)}, u32[]{:S(2)}, u32[]{:S(2)}) %collective-permute-start.1) | collective-permute-done | bytes 3145760 | tf_op jit(solution)/shard_map/ppermute | solution.py:17
  170.8 19.6 %copy.5 = f32[256,8,8,512]{3,1,2,0:T(8,128)} copy(bf16[256,8,8,512]{3,2,1,0:T(8,128)(2,1)} %bitcast.15) | data formatting | bytes 50331648
  190.4 50.9 %collective-permute-done.2 = bf16[768,2048]{1,0:T(8,128)(2,1)} collective-permute-done((bf16[768,2048]{1,0:T(8,128)(2,1)}, bf16[768,2048]{1,0:T(8,128)(2,1)}, u32[]{:S(2)}, u32[]{:S(2)}) %collective-permute-start.2) | collective-permute-done | bytes 3145760 | tf_op jit(solution)/shard_map/ppermute | solution.py:17
  241.3 4.0 constant_dynamic-update-slice_fusion.7
  245.3 4.2 constant_dynamic-update-slice_fusion.6
  249.4 3.9 constant_dynamic-update-slice_fusion.5
  253.4 1.9 constant_dynamic-update-slice_fusion.4
  255.3 3.9 constant_dynamic-update-slice_fusion.3
  259.2 4.0 constant_dynamic-update-slice_fusion.2
  263.2 2.2 constant_dynamic-update-slice_fusion.1
  265.4 1.9 constant_dynamic-update-slice_fusion
  267.3 62.7 %multiply_convert_fusion = bf16[2048,4096]{1,0:T(8,128)(2,1)} fusion(f32[2048,4096]{1,0:T(8,128)} %bitcast.14, bf16[3072,4096]{1,0:T(8,128)(2,1)} %all-gather.2.cloned.1.call-done, bf16[6144,2048]{1,0:T(8,128)(2,1)} %constant_dynamic-update-slice_fusion, s32[]{:T(128)S(6)} %select_n.18), kind=kOutput, calls=%fused_computation | convolution fusion | flops 51556384768 | bytes 88080384 | tf_op jit(solution)/shard_map/dot_general | solution.py:25
  330.1 61.0 %fusion.3 = f32[3072,2048]{1,0:T(8,128)} fusion(bf16[3072,4096]{1,0:T(8,128)(2,1)} %all-gather.2.cloned.1.call-done, bf16[2048,4096]{1,0:T(8,128)(2,1)} %multiply_convert_fusion), kind=kOutput, calls=%fused_computation.15 | convolution fusion | flops 51539607552 | bytes 67108864 | tf_op jit(solution)/shard_map/dot_general | solution.py:32
  391.0 0.0 reduce-scatter.5.cloned.1.call-start
  391.1 412.1 %reduce-scatter.3.cloned.1.call-done = f32[768,2048]{1,0:T(8,128)} async-done(((f32[3072,2048]{1,0:T(8,128)}), f32[768,2048]{1,0:T(8,128)}) %reduce-scatter.3.cloned.1.call-update) | async-done | bytes 6291472 | tf_op jit(solution)/shard_map/reduce_scatter | solution.py:31
  803.2 17.0 %convolution_bitcast_fusion = f32[3072,768]{0,1:T(8,128)} fusion(bf16[3072,2048]{1,0:T(8,128)(2,1)} %param.3, f32[768,2048]{1,0:T(8,128)} %reduce-scatter.3.cloned.1.call-done), kind=kOutput, calls=%fused_computation.2 | convolution fusion | flops 9665249280 | bytes 28311552 | tf_op jit(solution)/shard_map/dot_general | solution.py:41
  820.2 78.7 %reduce-scatter.5.cloned.1.call-done = f32[384,768]{0,1:T(8,128)} async-done(((f32[3072,768]{0,1:T(8,128)}), f32[384,768]{0,1:T(8,128)}) %reduce-scatter.5.cloned.1.call-update) | async-done | bytes 1179664 | tf_op jit(solution)/shard_map/reduce_scatter | solution.py:40
  898.9 2.7 copy.4
  (10 shorter events, 0.1 us)
Async XLA Ops:
  6.5 260.8 %all-gather.2.cloned.1.call-start = ((), (), s32[]{:S(2)}) async-start(), calls=%async_computation.2 | async-start | bytes 28311552 | tf_op jit(solution)/shard_map/all_gather | solution.py:24
  10.3 792.9 %reduce-scatter.3.cloned.1.call-start = ((), (), s32[]{:S(2)}) async-start(), calls=%async_computation.3 | async-start | bytes 31457280 | tf_op jit(solution)/shard_map/reduce_scatter | solution.py:31
  24.6 73.2 %collective-permute-start = (bf16[768,2048]{1,0:T(8,128)(2,1)S(1)}, bf16[768,2048]{1,0:T(8,128)(2,1)S(1)}, u32[]{:S(2)}, u32[]{:S(2)}) collective-permute-start(bf16[768,2048]{1,0:T(8,128)(2,1)S(1)} %convolution_convert_fusion), channel_id=1, source_target_pairs={{0,1},{1,2},{2,3},{3,0},{4,5},{5,6},{6,7},{7,4},{8,9},{9,10},{10,1... | collective-permute-start | bytes 9437192 | tf_op jit(solution)/shard_map/ppermute | solution.py:17
  97.9 1.7 copy-start
  99.6 71.2 %collective-permute-start.1 = (bf16[768,2048]{1,0:T(8,128)(2,1)S(1)}, bf16[768,2048]{1,0:T(8,128)(2,1)}, u32[]{:S(2)}, u32[]{:S(2)}) collective-permute-start(bf16[768,2048]{1,0:T(8,128)(2,1)S(1)} %collective-permute-done), channel_id=1, source_target_pairs={{0,1},{1,2},{2,3},{3,0},{4,5},{5,6},{6,7},{7,4},{8,9},{9,10},{10,1... | collective-permute-start | bytes 9437192 | tf_op jit(solution)/shard_map/ppermute | solution.py:17
  170.8 70.5 %collective-permute-start.2 = (bf16[768,2048]{1,0:T(8,128)(2,1)}, bf16[768,2048]{1,0:T(8,128)(2,1)}, u32[]{:S(2)}, u32[]{:S(2)}) collective-permute-start(bf16[768,2048]{1,0:T(8,128)(2,1)} %collective-permute-done.1), channel_id=1, source_target_pairs={{0,1},{1,2},{2,3},{3,0},{4,5},{5,6},{6,7},{7,4},{8,9},{9,10},{10,1... | collective-permute-start | bytes 9437192 | tf_op jit(solution)/shard_map/ppermute | solution.py:17
  245.3 17.9 %copy-start.1 = (bf16[768,2048]{1,0:T(8,128)(2,1)S(1)}, bf16[768,2048]{1,0:T(8,128)(2,1)}, u32[]{:S(2)}) copy-start(bf16[768,2048]{1,0:T(8,128)(2,1)} %copy-done) | copy-start | bytes 9437188
  391.0 507.9 %reduce-scatter.5.cloned.1.call-start = ((), (), s32[]{:S(2)}) async-start(), calls=%async_computation.4 | async-start | bytes 10616832 | tf_op jit(solution)/shard_map/reduce_scatter | solution.py:40
Sparse Core Ops, SparseCore 0:
  10.4 132.8 all-gather.1
  391.2 411.9 reduce-scatter.2
  820.3 78.5 reduce-scatter.4
